TPU v7x, 1024 devices: a whole 4x8x16 slice. The times are simulated.
1024 devices in a mesh: ep: 16 (over y_hi, x), edp: 16 (over z), tp: 4 (over y_lo, core).
Axes of the slice: x: 4, y: 8 (y_hi: 4, y_lo: 2; y = y_hi * 2 + y_lo), z: 16, core: 2. Of those that a mesh axis runs over, the one named last changes fastest.
Arguments:
- tokens: bfloat16 [32768, 4096], P(('ep', 'edp'), 'tp'), may hold values from -6 to 6
- cotangent: bfloat16 [32768, 4096], P(('ep', 'edp'), 'tp'), may hold values from -6 to 6
- expert_ids: int32 [32768, 8], P(('ep', 'edp')), may hold values from 0 to 127, all different within a row; in each aligned block of 128 rows (0 to 127, 128 to 255, ...) at most 10 rows name the same one
- route_weights: float32 [32768, 8], P(('ep', 'edp')), may hold values from 0.1 to 1
- expert_weights: bfloat16 [3, 6144, 4096], P(None, ('ep', 'tp')), may hold values from -0.15625 to 0.15625
Outputs:
- mixed: bfloat16 [32768, 4096], P(('ep', 'edp'), 'tp')
- grad_tokens: bfloat16 [32768, 4096], P(('ep', 'edp'), 'tp')
- weight_grads: float32 [3, 6144, 4096], P(None, ('ep', 'tp'), 'edp')
Inputs may be any that keep to these rules, and one draw needn't show every extreme that they name: `expert_ids`: each token names 8 different experts; within the tokens of one (ep, edp) index no expert is named by more than 10 tokens.
All inputs are finite; a program needn't handle non-finite values.
Results may differ from a plain program's by a relative error of at most 0.017.
Values may be sent and summed in bfloat16 or wider, within the bound.
No kernel may reach another device: no remote copies, remote signals or barrier semaphores. Data moves between devices by JAX's collectives and lax.ppermute only.
A program may use at most 64 MiB of HBM per device.

v0:
```python
import jax
import jax.numpy as jnp
from jax import lax
from jax.sharding import PartitionSpec as P

CAP = 10


def in_one_piece(arrays, axis, split_dim, concat_dim, along):
    both = jnp.concatenate(arrays, axis=along)
    result, at, finished = (
        lax.all_to_all(both, axis, split_axis=split_dim, concat_axis=concat_dim, tiled=True),
        0,
        [],
    )
    for a in arrays:
        finished.append(lax.slice_in_dim(result, at, at + a.shape[along], axis=along))
        at += a.shape[along]
    return tuple(finished)


def side_by_side(arrays, axis, dim, along):
    ends, at = ([], 0)
    for a in arrays[:-1]:
        at += a.shape[along]
        ends.append(at)
    both = jnp.concatenate(arrays, axis=along)
    return tuple(jnp.split(lax.all_gather(both, axis, axis=dim, tiled=True), ends, axis=along))


def split_up(x, dim, devices):
    shape = x.shape
    parts = x.reshape(*shape[:dim], devices, shape[dim] // devices, *shape[dim + 1 :])
    return jnp.moveaxis(parts, dim, 0)


def sum_at_owner(x, axis, dim):
    devices = lax.axis_size(axis)
    parts = lax.all_to_all(split_up(x, dim, devices), axis, 0, 0, tiled=True)
    return jnp.sum(parts.astype(jnp.float32), axis=0)


def sent_together(arrays, axis, dim, along):
    widths = [a.shape[along] for a in arrays]
    both = jnp.concatenate(arrays, axis=along)
    result = sum_at_owner(both, axis, dim)
    return tuple(jnp.split(result, [sum(widths[:k]) for k in range(1, len(widths))], axis=along))


def route_tables(expert_ids, route_weights, window):
    tok_rows, top_count = expert_ids.shape
    flat_ids = expert_ids.reshape(-1)
    matches = (flat_ids[:, None] == jnp.arange(window, dtype=jnp.int32)[None, :]).astype(jnp.int32)
    slot_index = jnp.sum(matches * (jnp.cumsum(matches, axis=0) - 1), axis=1)
    in_slot = (slot_index[:, None] == jnp.arange(CAP, dtype=jnp.int32)[None, :]).astype(jnp.float32)
    placed = matches.astype(jnp.float32)[:, :, None] * in_slot[:, None, :]
    placed = placed.reshape(tok_rows, top_count, window, CAP)
    select = jnp.sum(placed, axis=1)
    weighted = jnp.sum(placed * route_weights[:, :, None, None], axis=1)
    return (select, weighted)


def pack_rows(select, weighted, features, grads_in):
    packed = jnp.einsum(
        "tec,td->ecd", select.astype(jnp.bfloat16), features, preferred_element_type=jnp.float32
    ).astype(jnp.bfloat16)
    scaled = jnp.einsum(
        "tec,td->ecd", weighted, grads_in.astype(jnp.float32), precision=lax.Precision.HIGHEST
    ).astype(jnp.bfloat16)
    return (jnp.repeat(packed, 4, axis=0), jnp.repeat(scaled, 4, axis=0))


def shards(tokens, cotangent, expert_ids, route_weights, expert_weights):
    n_devices = lax.axis_size("ep")
    window = n_devices // 4
    select, weighted = route_tables(expert_ids, route_weights, window)
    packed, scaled = pack_rows(select, weighted, tokens, cotangent)
    slice_tokens, slice_grads = in_one_piece((packed, scaled), "ep", 0, 0, 1)
    rows_in, grads_in = side_by_side((slice_tokens, slice_grads), "tp", 2, 0)
    width = rows_in.shape[2]
    token_rows = rows_in.reshape(-1, width)
    grad_rows = grads_in.reshape(-1, width)
    gate_up = jnp.einsum(
        "rd,jfd->jrf", token_rows, expert_weights[:2], preferred_element_type=jnp.float32
    )
    gate_val = gate_up[0]
    up_val = gate_up[1]
    gate_weight = expert_weights[0]
    up_weight = expert_weights[1]
    down_weight = expert_weights[2]
    sigmoid_gate = jax.nn.sigmoid(gate_val)
    active = gate_val * sigmoid_gate
    hidden = (active * up_val).astype(jnp.bfloat16)
    out_part = jnp.dot(hidden, down_weight, preferred_element_type=jnp.float32)
    contract_last = (((1,), (1,)), ((), ()))
    d_hidden = lax.dot_general(
        grad_rows, down_weight, contract_last, preferred_element_type=jnp.float32
    )
    d_gate = (d_hidden * up_val * sigmoid_gate * (1.0 + gate_val * (1.0 - sigmoid_gate))).astype(
        jnp.bfloat16
    )
    d_up = (d_hidden * active).astype(jnp.bfloat16)
    back_part = jnp.dot(d_gate, gate_weight, preferred_element_type=jnp.float32) + jnp.dot(
        d_up, up_weight, preferred_element_type=jnp.float32
    )
    contract_rows = (((0,), (0,)), ((), ()))
    grad_gate = lax.dot_general(
        d_gate, token_rows, contract_rows, preferred_element_type=jnp.float32
    )
    grad_up = lax.dot_general(d_up, token_rows, contract_rows, preferred_element_type=jnp.float32)
    grad_down = lax.dot_general(
        hidden, grad_rows, contract_rows, preferred_element_type=jnp.float32
    )
    weight_grads = lax.psum_scatter(
        jnp.stack([grad_gate, grad_up, grad_down]).astype(jnp.bfloat16),
        "edp",
        scatter_dimension=2,
        tiled=True,
    ).astype(jnp.float32)
    out_sum, back_sum = sent_together(
        (out_part.astype(jnp.bfloat16), back_part.astype(jnp.bfloat16)), "tp", 1, 0
    )
    home_out, home_back = in_one_piece(
        (
            out_sum.astype(jnp.bfloat16).reshape(n_devices, CAP, -1),
            back_sum.astype(jnp.bfloat16).reshape(n_devices, CAP, -1),
        ),
        "ep",
        0,
        0,
        1,
    )
    pair_out = home_out.astype(jnp.float32).reshape(window, 4, CAP, -1).sum(axis=1)
    pair_back = home_back.astype(jnp.float32).reshape(window, 4, CAP, -1).sum(axis=1)
    mixed = jnp.einsum("tec,ecd->td", weighted, pair_out, precision=lax.Precision.HIGHEST).astype(
        jnp.bfloat16
    )
    grad_tokens = jnp.einsum(
        "tec,ecd->td", select, pair_back, precision=lax.Precision.HIGHEST
    ).astype(jnp.bfloat16)
    return (mixed, grad_tokens, weight_grads)


def solution(mesh):
    placed = (
        P(("ep", "edp"), "tp"),
        P(("ep", "edp"), "tp"),
        P(("ep", "edp"), None),
        P(("ep", "edp"), None),
        P(None, ("ep", "tp"), None),
    )
    return jax.shard_map(
        shards,
        mesh=mesh,
        in_specs=placed,
        out_specs=(P(("ep", "edp"), "tp"), P(("ep", "edp"), "tp"), P(None, ("ep", "tp"), "edp")),
        check_vma=False,
    )
```

profile of v0, /device:TPU:2, one launch (start us, length us, event | category | flops | bytes accessed | tf_op | source)
XLA Modules:
  0.0 222.8 jit_solution(4905263341049664303)
XLA Ops:
  7.2 0.0 all-gather.2.cloned.1.call-start
  7.2 0.7 convert_convert_fusion
  8.0 0.8 copy.19
  8.7 0.1 eq.61
  8.8 0.1 eq.57
  8.9 1.1 reduce-window.6
  10.1 0.2 slice_reduce_fusion
  10.3 0.2 reduce-window.9
  10.5 0.1 add_bitcast_fusion
  10.6 0.1 eq.65
  10.7 0.8 multiply_reduce_fusion
  11.6 0.2 convolution_convert_fusion.5
  11.7 1.2 convolution_convert_fusion.4
  12.9 0.1 broadcast_in_dim.5
  13.0 0.1 broadcast_in_dim.4
  13.1 0.2 pad_maximum_fusion.3
  13.3 31.9 %all_to_all.15 = bf16[16,20,1024]{2,1,0:T(8,128)(2,1)S(1)} all-to-all(bf16[16,20,1024]{2,1,0:T(8,128)(2,1)S(1)} %pad_maximum_fusion.3), channel_id=1, replica_groups=mesh['ep'=16,'edp'=16,'tp'=4] {'ep'}, dimensions={0} | all-to-all | bytes 1310720 | tf_op jit(solution)/shard_map/all_to_all | solution.py:12
  45.2 0.1 fusion.41
  45.3 1.1 pad_maximum_fusion.2
  46.5 60.3 %all-gather.2.cloned.1.call-done = bf16[32,10,4096]{2,1,0:T(8,128)(2,1)} async-done(((bf16[32,10,1024]{2,1,0:T(8,128)(2,1)}), bf16[32,10,4096]{2,1,0:T(8,128)(2,1)}) %all-gather.2.cloned.1.call-update) | async-done | bytes 2621456 | tf_op jit(solution)/shard_map/all_gather | solution.py:28
  106.8 3.9 %fusion.40 = (bf16[16,10,4096]{2,1,0:T(8,128)(2,1)S(1)}, bf16[16,10,4096]{2,1,0:T(8,128)(2,1)}) fusion(bf16[32,10,4096]{2,1,0:T(8,128)(2,1)} %all-gather.2.cloned.1.call-done), kind=kLoop, calls=%fused_computation.70 | loop fusion | bytes 5242880 | tf_op jit(solution)/shard_map/split | solution.py:28
  110.7 1.3 reshape.110
  112.0 1.3 reshape.125
  113.3 1.8 reshape.111
  115.2 2.7 %fusion.8 = f32[2,160,96]{2,1,0:T(8,128)S(1)} fusion(bf16[160,4096,1]{1,0,2:T(8,128)(2,1)} %reshape.125, bf16[3,96,4096]{2,1,0:T(8,128)(2,1)} %param.9), kind=kOutput, calls=%fused_computation.20 | convolution fusion | flops 251658240 | bytes 3006464 | tf_op jit(solution)/shard_map/rd,jfd->jrf/dot_general | solution.py:83
  117.9 0.5 fusion.31
  118.4 0.4 fusion.3
  118.8 0.5 convolution_convert_fusion
  119.3 0.5 fusion.12
  119.8 0.5 fusion
  120.3 0.3 pad_maximum_fusion
  120.6 1.9 copy.27
  122.5 4.7 %all-to-all-start.1 = ((bf16[4,320,1024]{2,1,0:T(8,128)(2,1)}), bf16[4,320,1024]{2,1,0:T(8,128)(2,1)}, u32[]{:S(2)}, u32[]{:S(2)}) async-start(bf16[4,320,1024]{2,1,0:T(8,128)(2,1)} %bitcast.114), calls=%async_computation.1 | async-start | bytes 5242880 | tf_op jit(solution)/shard_map/all_to_all | solution.py:39
  127.2 0.0 reduce-scatter.2.cloned.1.call-start
  127.2 0.4 fusion.2
  127.6 0.4 fusion.1
  128.0 1.7 pad_maximum_fusion.1
  129.8 28.7 %all-to-all-done.1 = bf16[4,320,1024]{2,1,0:T(8,128)(2,1)} async-done(((bf16[4,320,1024]{2,1,0:T(8,128)(2,1)}), bf16[4,320,1024]{2,1,0:T(8,128)(2,1)}, u32[]{:S(2)}, u32[]{:S(2)}) %all-to-all-start.1) | async-done | bytes 2621472 | tf_op jit(solution)/shard_map/all_to_all | solution.py:39
  158.5 2.3 %reduce = bf16[320,1024]{1,0:T(8,128)(2,1)S(1)} reduce(bf16[4,320,1024]{2,1,0:T(8,128)(2,1)} %all-to-all-done.1, bf16[]{:T(256)} %constant.18), dimensions={0}, to_apply=%region_5.6.clone | reduce | flops 983040 | bytes 3276802 | tf_op jit(solution)/shard_map/reduce_sum | solution.py:40
  160.9 0.1 reshape.113
  161.0 0.1 reshape.114
  161.1 1.1 pad_maximum_fusion.4
  162.2 9.1 %all-to-all-start.2 = ((bf16[16,20,1024]{2,1,0:T(8,128)(2,1)}), bf16[16,20,1024]{2,1,0:T(8,128)(2,1)S(1)}, u32[]{:S(2)}, u32[]{:S(2)}) async-start(bf16[16,20,1024]{2,1,0:T(8,128)(2,1)} %pad_maximum_fusion.4), calls=%async_computation.2 | async-start | bytes 1572864 | tf_op jit(solution)/shard_map/all_to_all | solution.py:12
  171.3 40.1 %reduce-scatter.2.cloned.1.call-done = bf16[3,96,256]{2,1,0:T(8,128)(2,1)} async-done(((bf16[3,96,4096]{2,1,0:T(8,128)(2,1)}), bf16[3,96,256]{2,1,0:T(8,128)(2,1)}) %reduce-scatter.2.cloned.1.call-update) | async-done | bytes 147472 | tf_op jit(solution)/shard_map/reduce_scatter | solution.py:114
  211.4 1.6 convert_element_type.87
  213.0 0.3 convert_reduce_fusion
  213.3 1.3 fusion.7
  214.6 1.3 fusion.6
  (15 shorter events, 0.2 us)
Async XLA Ops:
  7.2 4.4 %copy-start = (bf16[128,1024]{1,0:T(8,128)(2,1)S(1)}, bf16[128,1024]{1,0:T(8,128)(2,1)}, u32[]{:S(2)}) copy-start(bf16[128,1024]{1,0:T(8,128)(2,1)} %param.5) | copy-start | bytes 786436
  7.2 99.6 %all-gather.2.cloned.1.call-start = ((), (), s32[]{:S(2)}) async-start(), calls=%async_computation.4 | async-start | bytes 5242880 | tf_op jit(solution)/shard_map/all_gather | solution.py:28
  115.1 2.8 %copy-start.2 = (bf16[3,96,4096]{2,1,0:T(8,128)(2,1)S(1)}, bf16[3,96,4096]{2,1,0:T(8,128)(2,1)}, u32[]{:S(2)}) copy-start(bf16[3,96,4096]{2,1,0:T(8,128)(2,1)} %param.9) | copy-start | bytes 7077892
  122.5 4.7 %copy-start.1 = (bf16[160,4096]{1,0:T(8,128)(2,1)S(1)}, bf16[160,4096]{1,0:T(8,128)(2,1)}, u32[]{:S(2)}) copy-start(bf16[160,4096]{1,0:T(8,128)(2,1)} %reshape.110) | copy-start | bytes 3932164
  122.5 36.0 %all-to-all-start.1 = ((bf16[4,320,1024]{2,1,0:T(8,128)(2,1)}), bf16[4,320,1024]{2,1,0:T(8,128)(2,1)}, u32[]{:S(2)}, u32[]{:S(2)}) async-start(bf16[4,320,1024]{2,1,0:T(8,128)(2,1)} %bitcast.114), calls=%async_computation.1 | async-start | bytes 5242880 | tf_op jit(solution)/shard_map/all_to_all | solution.py:39
  127.2 84.2 %reduce-scatter.2.cloned.1.call-start = ((), (), s32[]{:S(2)}) async-start(), calls=%async_computation.5 | async-start | bytes 2506752 | tf_op jit(solution)/shard_map/reduce_scatter | solution.py:114
  162.2 50.8 %all-to-all-start.2 = ((bf16[16,20,1024]{2,1,0:T(8,128)(2,1)}), bf16[16,20,1024]{2,1,0:T(8,128)(2,1)S(1)}, u32[]{:S(2)}, u32[]{:S(2)}) async-start(bf16[16,20,1024]{2,1,0:T(8,128)(2,1)} %pad_maximum_fusion.4), calls=%async_computation.2 | async-start | bytes 1572864 | tf_op jit(solution)/shard_map/all_to_all | solution.py:12
Sparse Core Ops, SparseCore 0:
  46.6 60.1 all-gather.1
  131.4 79.9 reduce-scatter.1
where the time goes:
time: 223 us
  waiting for transfers between devices  129 us (58%)
  blocking collectives  31.9 us (14%)
  between operations  14.3 us (6%)
  starting transfers between devices  13.8 us (6%)
  local copies, waits for them, and re-layouts  12.1 us (5%)
  other arithmetic  11.7 us (5%)
  matrix products  9.92 us (4%)
    all_gather x1, waiting for transfers between devices, side_by_side(): lax.all_gather(both, axis, axis=dim, tiled=True)  60.3 us
    reduce_scatter x1, waiting for transfers between devices, shards(): lax.psum_scatter(jnp.stack([grad_gate, grad_up, grad_down]).astype(jnp.bf...  40.1 us
    all_to_all x1, blocking collectives, in_one_piece(): lax.all_to_all(both, axis, split_axis=split_dim, concat_axis=concat_dim,...  31.9 us
    all_to_all x1, waiting for transfers between devices, sum_at_owner(): parts = lax.all_to_all(split_up(x, dim, devices), axis, 0, 0, tiled=True)  28.7 us
    all_to_all x1, starting transfers between devices, in_one_piece(): lax.all_to_all(both, axis, split_axis=split_dim, concat_axis=concat_dim,...  9.09 us
    all_to_all x1, starting transfers between devices, sum_at_owner(): parts = lax.all_to_all(split_up(x, dim, devices), axis, 0, 0, tiled=True)  4.67 us
  transfers between devices with their start and end apart: 4, of which 3 were waited for; matrix products, arithmetic and copies ran while one was open for 4% of the time, Pallas kernels for 0%

commit v1 on v0

v1 whole, which is shorter than its diff:
```python
import functools

import jax
import jax.numpy as jnp
from jax import lax
from jax.experimental import pallas as pl
from jax.experimental.pallas import tpu as pltpu
from jax.sharding import Mesh, PartitionSpec as P

HALF = 12
BLOCK = 2 * HALF
F32, BF16 = jnp.float32, jnp.bfloat16
VMEM = pl.BlockSpec(memory_space=pltpu.VMEM)
SMEM = pl.BlockSpec(memory_space=pltpu.SMEM)


def dot(a, b, contract, **kw):
    return lax.dot_general(a, b, ((contract[:1], contract[1:]), ((), ())), preferred_element_type=F32, **kw)


def pack_kernel(copies, ids_ref, wts_ref, tok_ref, cot_ref, out_ref, sel_ref, selw_ref):
    window = out_ref.shape[0]
    n_tok = tok_ref.shape[0]
    ids = ids_ref[...]
    wts = wts_ref[...]
    rows = [jnp.max((ids == e).astype(F32), axis=0, keepdims=True) for e in range(window)]
    named = jnp.concatenate(rows + [jnp.zeros((8 - window, n_tok), F32)], axis=0)
    before = lax.broadcasted_iota(jnp.int32, (n_tok, n_tok), 0) < lax.broadcasted_iota(jnp.int32, (n_tok, n_tok), 1)
    rank = dot(named.astype(BF16), before.astype(BF16), (1, 0)).astype(jnp.int32)
    row = lax.broadcasted_iota(jnp.int32, (BLOCK, n_tok), 0)
    slot = jnp.where(row < HALF, row, row - HALF)
    tok = tok_ref[...]
    cot = cot_ref[...]
    for e in range(window):
        hit = jnp.logical_and(slot == rank[e : e + 1], named[e : e + 1] > 0.5)
        weight = jnp.sum(jnp.where(ids == e, wts, 0.0), axis=0, keepdims=True)
        pick_tok = jnp.where(jnp.logical_and(hit, row < HALF), 1.0, 0.0)
        pick_cot = jnp.where(jnp.logical_and(hit, row >= HALF), 1.0, 0.0)
        selw = pick_cot * weight
        scale = jnp.where(row[:, :1] < HALF, 1.0, jnp.sum(selw, axis=1, keepdims=True))
        picked = dot(pick_tok.astype(BF16), tok, (1, 0)) + dot(pick_cot.astype(BF16), cot, (1, 0))
        block = (picked * scale).astype(BF16)
        for k in range(copies):
            out_ref[e, k] = block
        sel_ref[e * BLOCK : (e + 1) * BLOCK] = pick_tok
        selw_ref[e * BLOCK : (e + 1) * BLOCK] = selw


def expert_kernel(core_ref, own_ref, other_ref, w_ref, y_own_ref, y_other_ref, g_ref):
    core = core_ref[0]
    n_src, n_yl, _, width = own_ref.shape
    n_rows = n_src * BLOCK
    hid = w_ref.shape[1]
    blocks = []
    for yl in range(n_yl):
        blocks.append((own_ref, y_own_ref, yl, 2 * yl + core))
        blocks.append((other_ref, y_other_ref, yl, 2 * yl + 1 - core))

    def weights(t):
        cols = pl.ds(pl.multiple_of(t * width, width), width)
        return w_ref[:, :, cols].reshape(3 * hid, width)

    proj = jnp.zeros((3 * hid, n_rows), F32)
    for x_ref, _, yl, t in blocks:
        proj = proj + dot(weights(t), x_ref[:, yl].reshape(n_rows, width), (1, 1))
    lane = lax.broadcasted_iota(jnp.int32, (hid, n_rows), 1)
    live = lax.rem(lane, BLOCK) < HALF
    gate = proj[:hid]
    up = proj[hid : 2 * hid]
    d_hidden = pltpu.roll(proj[2 * hid :], n_rows - HALF, 1)
    sig = jax.nn.sigmoid(gate)
    active = gate * sig
    hidden = jnp.where(live, active * up, 0.0)
    d_gate = jnp.where(live, d_hidden * up * sig * (1.0 + gate * (1.0 - sig)), 0.0)
    d_up = jnp.where(live, d_hidden * active, 0.0)
    left = jnp.concatenate([d_gate, d_up, pltpu.roll(hidden, HALF, 1)], axis=0)
    left_t = left.T.astype(BF16)
    left = left.astype(BF16)
    for x_ref, y_ref, yl, t in blocks:
        cols = pl.ds(pl.multiple_of(t * width, width), width)
        grad = dot(left, x_ref[:, yl].reshape(n_rows, width), (1, 0))
        g_ref[:, :, cols] = grad.astype(BF16).reshape(3, hid, width)
        y = dot(left_t, weights(t), (1, 0))
        y_ref[:, yl] = y.astype(BF16).reshape(n_src, BLOCK, width)


def combine_kernel(z_ref, sel_ref, selw_ref, mixed_ref, grad_ref):
    window, copies = z_ref.shape[:2]
    total = z_ref[:, 0].astype(F32)
    for k in range(1, copies):
        total = total + z_ref[:, k].astype(F32)
    total = total.reshape(window * BLOCK, z_ref.shape[3])
    exact = dict(precision=lax.Precision.HIGHEST)
    mixed_ref[...] = dot(selw_ref[...], total, (0, 0), **exact).astype(BF16)
    grad_ref[...] = dot(sel_ref[...], total, (0, 0), **exact).astype(BF16)


def call(kernel, out_shapes, args, smem=0):
    return pl.pallas_call(
        kernel,
        out_shape=[jax.ShapeDtypeStruct(s, d) for s, d in out_shapes],
        in_specs=[SMEM] * smem + [VMEM] * (len(args) - smem),
        out_specs=[VMEM] * len(out_shapes),
        compiler_params=pltpu.CompilerParams(vmem_limit_bytes=48 * 1024 * 1024),
    )(*args)


def shards(tokens, cotangent, expert_ids, route_weights, expert_weights):
    n_yh, n_x, n_yl = (lax.axis_size(a) for a in ("yh", "x", "yl"))
    window = n_yh
    n_tok, width = tokens.shape
    plane = ("yh", "x", "yl")
    copies = n_x * n_yl
    n_src = n_yh * n_x
    swap = [(0, 1), (1, 0)]

    packed, sel, selw = call(
        functools.partial(pack_kernel, copies),
        [((window, copies, BLOCK, width), BF16)] + [((window * BLOCK, n_tok), F32)] * 2,
        (expert_ids.T, route_weights.T, tokens, cotangent),
    )
    own = lax.all_to_all(packed.reshape(-1, BLOCK, width), plane, 0, 0, tiled=True)
    other = lax.ppermute(own, "c", swap)
    shape = (n_src, n_yl, BLOCK, width)
    core = lax.axis_index("c").astype(jnp.int32).reshape(1)
    y_own, y_other, grads = call(
        expert_kernel,
        [(shape, BF16), (shape, BF16), (expert_weights.shape, BF16)],
        (core, own.reshape(shape), other.reshape(shape), expert_weights),
        smem=1,
    )
    weight_grads = lax.psum_scatter(grads, "z", scatter_dimension=2, tiled=True).astype(F32)
    partner = lax.ppermute(y_other, "c", swap)
    y = (y_own.astype(F32) + partner.astype(F32)).astype(BF16)
    home = lax.all_to_all(y.reshape(-1, BLOCK, width), plane, 0, 0, tiled=True)
    mixed, grad_tokens = call(
        combine_kernel,
        [((n_tok, width), BF16)] * 2,
        (home.reshape(window, copies, BLOCK, width), sel, selw),
    )
    return mixed, grad_tokens, weight_grads


def solution(mesh):
    n_ep, n_edp, n_tp = mesh.devices.shape
    side = 4
    fine = Mesh(
        mesh.devices.reshape(side, n_ep // side, n_edp, n_tp // 2, 2), ("yh", "x", "z", "yl", "c")
    )
    group, feat = ("yh", "x", "z"), ("yl", "c")
    hid = ("yh", "x", "yl", "c")
    placed = (P(group, feat), P(group, feat), P(group, None), P(group, None), P(None, hid, None))
    return jax.shard_map(
        shards,
        mesh=fine,
        in_specs=placed,
        out_specs=(P(group, feat), P(group, feat), P(None, hid, "z")),
        check_vma=False,
    )
```

time: 223 us -> 168 us (0.75)
  the two profiles are of different devices: /device:TPU:2 before, /device:TPU:4 now
where the time goes in v1:
time: 168 us; the launch traced here: 167 us
  blocking collectives  94.2 us (56%)
  waiting for transfers between devices  37.9 us (23%)
  between operations  14.1 us (8%)
  Pallas kernels  10.5 us (6%)
  local copies, waits for them, and re-layouts  4.44 us (3%)
  starting transfers between devices  3.98 us (2%)
  other arithmetic  2.35 us (1%)
    all_to_all x1, blocking collectives, shards(): lax.all_to_all(packed.reshape(-1, BLOCK, width), plane, 0, 0, tiled=True)  49.4 us
    all_to_all x1, blocking collectives, shards(): home = lax.all_to_all(y.reshape(-1, BLOCK, width), plane, 0, 0, tiled=True)  44.8 us
    reduce_scatter x1, waiting for transfers between devices, shards(): lax.psum_scatter(grads, 'z', scatter_dimension=2, tiled=True).astype(F32)  31.1 us
    pallas_call x3, Pallas kernels, call(): pl.pallas_call(kernel, out_shape=[jax.ShapeDtypeStruct(s, d) for s, d in...  10.5 us
    unnamed x10, local copies, waits for them, and re-layouts  4.44 us
    ppermute x1, waiting for transfers between devices, shards(): partner = lax.ppermute(y_other, 'c', swap)  3.43 us
    ppermute x1, waiting for transfers between devices, shards(): other = lax.ppermute(own, 'c', swap)  3.37 us
  transfers between devices with their start and end apart: 3, of which 3 were waited for; matrix products, arithmetic and copies ran while one was open for 0% of the time, Pallas kernels for 1%

profile of v1, /device:TPU:4, one launch (start us, length us, event | category | flops | bytes accessed | tf_op | source)
XLA Modules:
  0.0 167.5 jit_solution(7853203510677054501)
XLA Ops:
  7.2 0.0 reduce-scatter.2.cloned.1.call-start
  7.2 0.0 copy-start
  7.2 0.9 copy-done
  8.2 0.0 copy-start.1
  8.2 0.9 copy-done.1
  9.1 0.0 copy-start.2
  9.1 0.7 copy-done.2
  9.8 0.0 copy-start.3
  9.8 0.7 copy-done.3
  10.5 0.6 shard_map.76
  11.1 49.4 %all_to_all.10 = bf16[32,24,1024]{2,1,0:T(8,128)(2,1)S(1)} all-to-all(bf16[32,24,1024]{2,1,0:T(8,128)(2,1)S(1)} %bitcast.10), channel_id=1, replica_groups=mesh['yh'=4,'x'=4,'z'=16,'yl'=2,'c'=2] {'yh','x','yl'}, dimensions={0} | all-to-all | bytes 3145728 | tf_op jit(solution)/shard_map/all_to_all | solution.py:122
  60.4 1.9 %collective-permute-start = (bf16[32,24,1024]{2,1,0:T(8,128)(2,1)S(1)}, bf16[32,24,1024]{2,1,0:T(8,128)(2,1)S(1)}, u32[]{:S(2)}, u32[]{:S(2)}) collective-permute-start(bf16[32,24,1024]{2,1,0:T(8,128)(2,1)S(1)} %all_to_all.10), channel_id=1, source_target_pairs={{0,1},{1,0},{2,3},{3,2},{4,5},{5,4},{6,7},{7,6},{8,9},{9,8},{10,11... | collective-permute-start | bytes 4718600 | tf_op jit(solution)/shard_map/ppermute | solution.py:123
  62.3 3.4 %collective-permute-done = bf16[32,24,1024]{2,1,0:T(8,128)(2,1)S(1)} collective-permute-done((bf16[32,24,1024]{2,1,0:T(8,128)(2,1)S(1)}, bf16[32,24,1024]{2,1,0:T(8,128)(2,1)S(1)}, u32[]{:S(2)}, u32[]{:S(2)}) %collective-permute-start) | collective-permute-done | bytes 1572896 | tf_op jit(solution)/shard_map/ppermute | solution.py:123
  65.7 0.0 copy-start.4
  65.7 1.2 copy-done.4
  66.9 8.2 %shard_map.77 = (bf16[16,2,24,1024]{3,2,1,0:T(8,128)(2,1)S(1)}, bf16[16,2,24,1024]{3,2,1,0:T(8,128)(2,1)}, bf16[3,96,4096]{2,1,0:T(8,128)(2,1)}) custom-call(s32[1]{0:T(128)} %bitcast.core_ref, bf16[16,2,24,1024]{3,2,1,0:T(8,128)(2,1)S(1)} %bitcast.9, bf16[16,2,24,1024]{3,2,1,0:T(8,128)(2,1)} %bitcast.14, bf16[3,96,4096]{2,1,0:T(8,128)(2,1)} %w_ref.1), custom_call_target="tpu_custom_call" | custom-call | tf_op jit(solution)/shard_map/pallas_call | solution.py:99
  75.0 2.0 %collective-permute-start.1 = (bf16[16,2,24,1024]{3,2,1,0:T(8,128)(2,1)}, bf16[16,2,24,1024]{3,2,1,0:T(8,128)(2,1)S(1)}, u32[]{:S(2)}, u32[]{:S(2)}) collective-permute-start(bf16[16,2,24,1024]{3,2,1,0:T(8,128)(2,1)} %get-tuple-element.13), channel_id=1, source_target_pairs={{0,1},{1,0},{2,3},{3,2},{4,5},{5,4},{6,7},{7,6},{8,9},{9,8},{10,11... | collective-permute-start | bytes 4718600 | tf_op jit(solution)/shard_map/ppermute | solution.py:133
  77.1 0.0 reduce-scatter.2.cloned.1.call-update
  77.1 3.4 %collective-permute-done.1 = bf16[16,2,24,1024]{3,2,1,0:T(8,128)(2,1)S(1)} collective-permute-done((bf16[16,2,24,1024]{3,2,1,0:T(8,128)(2,1)}, bf16[16,2,24,1024]{3,2,1,0:T(8,128)(2,1)S(1)}, u32[]{:S(2)}, u32[]{:S(2)}) %collective-permute-start.1) | collective-permute-done | bytes 1572896 | tf_op jit(solution)/shard_map/ppermute | solution.py:133
  80.5 0.7 add_convert_fusion
  81.3 44.8 %all_to_all.11 = bf16[32,24,1024]{2,1,0:T(8,128)(2,1)S(1)} all-to-all(bf16[32,24,1024]{2,1,0:T(8,128)(2,1)S(1)} %bitcast.13), channel_id=1, replica_groups=mesh['yh'=4,'x'=4,'z'=16,'yl'=2,'c'=2] {'yh','x','yl'}, dimensions={0} | all-to-all | bytes 3145728 | tf_op jit(solution)/shard_map/all_to_all | solution.py:135
  126.1 1.8 %shard_map.78 = (bf16[128,1024]{1,0:T(8,128)(2,1)}, bf16[128,1024]{1,0:T(8,128)(2,1)}) custom-call(bf16[4,8,24,1024]{3,2,1,0:T(8,128)(2,1)S(1)} %bitcast.8, f32[96,128]{1,0:T(8,128)S(1)} %get-tuple-element.14.sel_ref, f32[96,128]{1,0:T(8,128)S(1)} %get-tuple-element.15.selw_ref), custom_call_target="tpu_custom_call" | custom-call | tf_op jit(solution)/shard_map/pallas_call | solution.py:99
  127.9 31.1 %reduce-scatter.2.cloned.1.call-done = bf16[3,96,256]{2,1,0:T(8,128)(2,1)} async-done(((bf16[3,96,4096]{2,1,0:T(8,128)(2,1)}), bf16[3,96,256]{2,1,0:T(8,128)(2,1)}) %reduce-scatter.2.cloned.1.call-update) | async-done | bytes 147472 | tf_op jit(solution)/shard_map/reduce_scatter | solution.py:132
  159.0 1.6 convert_element_type.15
Async XLA Ops:
  7.2 151.8 %reduce-scatter.2.cloned.1.call-start = ((), (), s32[]{:S(2)}) async-start(), calls=%async_computation.3 | async-start | bytes 2506752 | tf_op jit(solution)/shard_map/reduce_scatter | solution.py:132
  7.2 1.0 copy-start
  8.2 0.9 copy-start.1
  9.1 0.7 copy-start.2
  9.8 0.7 copy-start.3
  60.4 5.3 %collective-permute-start = (bf16[32,24,1024]{2,1,0:T(8,128)(2,1)S(1)}, bf16[32,24,1024]{2,1,0:T(8,128)(2,1)S(1)}, u32[]{:S(2)}, u32[]{:S(2)}) collective-permute-start(bf16[32,24,1024]{2,1,0:T(8,128)(2,1)S(1)} %all_to_all.10), channel_id=1, source_target_pairs={{0,1},{1,0},{2,3},{3,2},{4,5},{5,4},{6,7},{7,6},{8,9},{9,8},{10,11... | collective-permute-start | bytes 4718600 | tf_op jit(solution)/shard_map/ppermute | solution.py:123
  65.7 1.2 copy-start.4
  75.0 5.5 %collective-permute-start.1 = (bf16[16,2,24,1024]{3,2,1,0:T(8,128)(2,1)}, bf16[16,2,24,1024]{3,2,1,0:T(8,128)(2,1)S(1)}, u32[]{:S(2)}, u32[]{:S(2)}) collective-permute-start(bf16[16,2,24,1024]{3,2,1,0:T(8,128)(2,1)} %get-tuple-element.13), channel_id=1, source_target_pairs={{0,1},{1,0},{2,3},{3,2},{4,5},{5,4},{6,7},{7,6},{8,9},{9,8},{10,11... | collective-permute-start | bytes 4718600 | tf_op jit(solution)/shard_map/ppermute | solution.py:133
Sparse Core Ops, SparseCore 0:
  77.2 81.6 reduce-scatter.1
